TPU v7x, 32 devices: a whole 2x2x4 slice. The times are simulated.
32 devices in a mesh: job: 2 (over y), row: 4 (over z), col: 2 (over x), samp: 2 (over core).
Axes of the slice: x: 2, y: 2, z: 4, core: 2. Of those that a mesh axis runs over, the one named last changes fastest.
Arguments:
- pair_repr: bfloat16 [256, 128, 128], P(('job', 'row'), ('col', 'samp')), parts along dimension 0, may hold values from -100 to 100
- asym_id: int32 [256], P('job'), parts along dimension 0, may hold values from 0 to 7, never falling along the last dimension, each value on 1 to 32 neighbouring positions
- valid_len: int32 [2], P('job'), parts along dimension 0, may hold values from 64 to 128
- rel_embed: bfloat16 [128, 128], replicated, may hold values from -12 to 12
- pair_gain: float32 [128], replicated, may hold values from 0.25 to 1.75
- bias_weight: bfloat16 [128, 16], replicated, may hold values from -64 to 64
- tokens: bfloat16 [32, 128, 768], P(('job', 'col', 'samp'), 'row'), parts along dimension 0, may hold values from -6 to 6
- token_gain: float32 [1, 768], replicated, may hold values from 0.25 to 1.75
- qkv_weight: bfloat16 [1, 3, 768, 768], P(None, None, None, 'row'), may hold values from -0.21875 to 0.21875
- out_weight: bfloat16 [1, 768, 768], P(None, 'row'), may hold values from -0.21875 to 0.21875
Outputs:
- refined: bfloat16 [32, 128, 768], P(('job', 'col', 'samp'), 'row'), parts along dimension 0
There are 2 independent parts, one for each index of `job`. A program takes and returns all parts, laid end to end along the dimension named above; an argument that names none is the same for every part. Nothing has to cross between parts.
Inputs may be any that keep to these rules, and one draw needn't show every extreme that they name: `asym_id`: chain indices never fall along the tokens.
All inputs are finite; a program needn't handle non-finite values.
Results may differ from a plain program's by a relative error of at most 0.002.
The roundings to bfloat16 on the way count: a program that leaves them out, or rounds other values in their place, can miss the bound.
Values may be sent and summed in bfloat16 or wider, within the bound.
A program may use at most 64 MiB of HBM per device.

v0:
```python
import functools
import math

import jax
import jax.numpy as jnp
from jax import lax
from jax.experimental import pallas as pl
from jax.experimental.pallas import tpu as pltpu
from jax.sharding import PartitionSpec as P

HEAD_DIM = 48
EPSILON = 1e-05
LANES = 128
MESH = pl.DeviceIdType.MESH


def normalize(values, gain_vector):
    average = jnp.mean(values, axis=-1, keepdims=True)
    centered = values - average
    variance = jnp.mean(centered * centered, axis=-1, keepdims=True)
    return centered * lax.rsqrt(variance + EPSILON) * gain_vector


def kernel(
    axes,
    split,
    asym_hbm,
    valid_hbm,
    pair_hbm,
    rel_hbm,
    pair_gain_hbm,
    bias_weight_hbm,
    tokens_hbm,
    token_gain_hbm,
    qkv_hbm,
    out_weight_hbm,
    out,
    asym,
    valid,
    pair,
    rel,
    pair_gain,
    bias_weight,
    token_gain,
    qkv,
    tok,
    ow,
    bias_send,
    bias_recv,
    bias,
    query,
    key,
    value,
    attended,
    heads_in,
    local_sem,
    tok_local,
    tok_send,
    tok_recv,
    bz_send,
    bz_recv,
    bp_send,
    bp_recv,
    own_bias_sem,
    oz_send,
    oz_recv,
    op_send,
    op_recv,
    at_send,
    at_recv,
):
    n_job, n_row, n_col, n_samp = axes
    job, me = lax.axis_index("job"), lax.axis_index("row")
    col, samp = lax.axis_index("col"), lax.axis_index("samp")
    samples, token_rows, width = tokens_hbm.shape
    total = n_row * token_rows
    tile_rows, tile_cols, channels = pair.shape
    bins = rel.shape[0]
    n_plane = n_col * n_samp
    plane = col * n_samp + samp
    all_heads = bias_weight.shape[0]
    local_heads = all_heads // n_row
    head_rows = bias_recv.shape[2]
    fold = LANES // tile_cols
    stripes = tile_rows // fold
    out_rows = ow.shape[1]
    row_pieces, col_pieces = split
    pieces = row_pieces * col_pieces
    piece_rows, piece_cols = out_rows // row_pieces, width // col_pieces
    shared = pieces > 1
    group = (job * n_samp + samp if row_pieces > 1 else 0) * col_pieces + (
        col if col_pieces > 1 else 0
    )
    local_width = local_heads * HEAD_DIM

    def row_peer(k):
        return lax.rem(me + k, n_row)

    def plane_peer(k):
        other = lax.rem(plane + k, n_plane)
        return {"col": lax.div(other, n_samp), "samp": lax.rem(other, n_samp)}, other

    def group_peer(k):
        other = lax.rem(group + k, pieces)
        device, held = {}, lax.div(other, col_pieces)
        if row_pieces > 1:
            device.update(job=lax.div(held, n_samp), samp=lax.rem(held, n_samp))
        if col_pieces > 1:
            device.update(col=lax.rem(other, col_pieces))
        return device, other

    loads = {}
    for index, (name, source, target) in enumerate(
        (
            ("asym", asym_hbm, asym),
            ("valid", valid_hbm, valid),
            ("pair", pair_hbm, pair),
            ("rel", rel_hbm, rel),
            ("pair_gain", pair_gain_hbm, pair_gain),
            ("bias_weight", bias_weight_hbm, bias_weight),
            ("token_gain", token_gain_hbm, token_gain),
            ("qkv", qkv_hbm.at[0], qkv),
            ("ow", out_weight_hbm.at[0], ow.at[me]),
        )
    ):
        loads[name] = pltpu.make_async_copy(source, target, local_sem.at[index])
    tok_loads = [
        pltpu.make_async_copy(tokens_hbm.at[s], tok.at[s, me], tok_local.at[s]) for s in range(samples)
    ]
    tok_loads[0].start()
    for name in ("asym", "pair", "rel", "pair_gain", "bias_weight", "valid"):
        loads[name].start()
    for s in range(1, samples):
        tok_loads[s].start()
    for name in ("token_gain", "qkv", "ow"):
        loads[name].start()

    barrier = pltpu.get_barrier_semaphore()
    for k in range(1, n_row):
        pl.semaphore_signal(barrier, inc=1, device_id={"row": row_peer(k)}, device_id_type=MESH)
    for k in range(1, n_plane):
        pl.semaphore_signal(barrier, inc=1, device_id=plane_peer(k)[0], device_id_type=MESH)
    if shared:
        for k in range(1, pieces):
            pl.semaphore_signal(barrier, inc=1, device_id=group_peer(k)[0], device_id_type=MESH)
    pl.semaphore_wait(barrier, (n_row - 1) + (n_plane - 1) + ((pieces - 1) if shared else 0))

    has_right, has_left = me < n_row - 1, me > 0
    right, left = jnp.minimum(me + 1, n_row - 1), jnp.maximum(me - 1, 0)

    def tok_copy(s, source, direction):
        return pltpu.make_async_remote_copy(
            src_ref=tok.at[s, source],
            dst_ref=tok.at[s, source],
            send_sem=tok_send.at[direction, s, source],
            recv_sem=tok_recv.at[s, source],
            device_id={"row": left if direction else right},
            device_id_type=MESH,
        )

    def send_own(s):
        tok_loads[s].wait()

        @pl.when(has_right)
        def _():
            tok_copy(s, me, 0).start()

        @pl.when(has_left)
        def _():
            tok_copy(s, me, 1).start()

    def pass_on(k, s):
        @pl.when(me - k >= 0)
        def _():
            source = jnp.maximum(me - k, 0)
            tok_copy(s, source, 0).wait_recv()

            @pl.when(has_right)
            def _():
                tok_copy(s, source, 0).start()

        @pl.when(me + k < n_row)
        def _():
            source = jnp.minimum(me + k, n_row - 1)
            tok_copy(s, source, 1).wait_recv()

            @pl.when(has_left)
            def _():
                tok_copy(s, source, 1).start()

    def finish_tok_sends(s):
        for k in range(0, n_row):

            @pl.when(jnp.logical_and(me - k >= 0, has_right))
            def _():
                tok_copy(s, jnp.maximum(me - k, 0), 0).wait_send()

            @pl.when(jnp.logical_and(me + k < n_row, has_left))
            def _():
                tok_copy(s, jnp.minimum(me + k, n_row - 1), 1).wait_send()

    for s in range(samples):
        send_own(s)

    for name in ("asym", "pair", "rel", "pair_gain", "bias_weight", "valid"):
        loads[name].wait()
    first_row, first_col = me * tile_rows, plane * tile_cols
    sub = lax.broadcasted_iota(jnp.int32, (tile_cols, LANES), 0)
    lane = lax.broadcasted_iota(jnp.int32, (tile_cols, LANES), 1)
    col_chain = jnp.zeros((tile_cols, LANES), jnp.int32)
    for j in range(tile_cols):
        col_chain = jnp.where(sub == j, asym[first_col + j], col_chain)
    reach = bins // 2 - 1
    turned_weight = bias_weight[...]
    for t in range(stripes):
        hots, rows = [], []
        for q in range(fold):
            i = q * stripes + t
            offset = jnp.clip(first_row + i - first_col - sub, -reach, reach) + reach
            bin_ids = jnp.where(col_chain == asym[first_row + i], offset, bins - 1)
            hots.append(jnp.where(bin_ids == lane, 1.0, 0.0).astype(jnp.bfloat16))
            rows.append(pair[i].astype(jnp.float32))
        summed = jnp.concatenate(rows, axis=0) + jnp.dot(
            jnp.concatenate(hots, axis=0), rel[...], preferred_element_type=jnp.float32
        )
        normed = normalize(summed, pair_gain[...]).astype(jnp.bfloat16)
        projected = lax.dot_general(
            turned_weight, normed, (((1,), (1,)), ((), ())), preferred_element_type=jnp.float32
        )
        bias_send[pl.ds(t, all_heads, stride=stripes), :] = projected

    def bias_part(dest):
        return bias_send.at[pl.ds(pl.multiple_of(dest * head_rows, head_rows), head_rows)]

    def bias_row_copy(k):
        dest = row_peer(k)
        return pltpu.make_async_remote_copy(
            src_ref=bias_part(dest),
            dst_ref=bias_recv.at[me, plane],
            send_sem=bz_send.at[k],
            recv_sem=bz_recv.at[k],
            device_id={"row": dest},
            device_id_type=MESH,
        )

    def bias_plane_copy(k, m):
        device, _ = plane_peer(m)
        source = row_peer(n_row - k)
        return pltpu.make_async_remote_copy(
            src_ref=bias_part(me) if k == 0 else bias_recv.at[source, plane],
            dst_ref=bias_recv.at[source, plane],
            send_sem=bp_send.at[k, m],
            recv_sem=bp_recv.at[k, m],
            device_id=device,
            device_id_type=MESH,
        )

    def bias_plane_wait(k, m):
        source = row_peer(n_row - k)
        origin = lax.rem(plane + n_plane - m, n_plane)
        pltpu.make_async_remote_copy(
            src_ref=bias_recv.at[source, origin],
            dst_ref=bias_recv.at[source, origin],
            send_sem=bp_send.at[k, m],
            recv_sem=bp_recv.at[k, m],
            device_id=plane_peer(m)[0],
            device_id_type=MESH,
        ).wait_recv()

    def bias_row_wait(k):
        source = row_peer(n_row - k)
        pltpu.make_async_remote_copy(
            src_ref=bias_recv.at[source, plane],
            dst_ref=bias_recv.at[source, plane],
            send_sem=bz_send.at[k],
            recv_sem=bz_recv.at[k],
            device_id={"row": row_peer(k)},
            device_id_type=MESH,
        ).wait_recv()

    for k in range(1, n_row):
        bias_row_copy(k).start()
    own_bias = pltpu.make_async_copy(bias_part(me), bias_recv.at[me, plane], own_bias_sem)
    own_bias.start()
    for m in range(1, n_plane):
        bias_plane_copy(0, m).start()

    def ow_part(source, piece):
        if not shared:
            return ow.at[source]
        first = pl.multiple_of(lax.div(piece, col_pieces) * piece_rows, piece_rows)
        start = pl.multiple_of(lax.rem(piece, col_pieces) * piece_cols, piece_cols)
        return ow.at[source, pl.ds(first, piece_rows), pl.ds(start, piece_cols)]

    def ow_row_copy(k):
        return pltpu.make_async_remote_copy(
            src_ref=ow_part(me, group),
            dst_ref=ow_part(me, group),
            send_sem=oz_send.at[k],
            recv_sem=oz_recv.at[k],
            device_id={"row": row_peer(k)},
            device_id_type=MESH,
        )

    def ow_row_wait(k):
        source = row_peer(n_row - k)
        pltpu.make_async_remote_copy(
            src_ref=ow_part(source, group),
            dst_ref=ow_part(source, group),
            send_sem=oz_send.at[k],
            recv_sem=oz_recv.at[k],
            device_id={"row": row_peer(k)},
            device_id_type=MESH,
        ).wait_recv()

    def ow_group_copy(k, m):
        source = row_peer(n_row - k)
        return pltpu.make_async_remote_copy(
            src_ref=ow_part(source, group),
            dst_ref=ow_part(source, group),
            send_sem=op_send.at[k, m],
            recv_sem=op_recv.at[k, m],
            device_id=group_peer(m)[0],
            device_id_type=MESH,
        )

    def ow_group_wait(k, m):
        source = row_peer(n_row - k)
        origin = lax.rem(group + pieces - m, pieces)
        pltpu.make_async_remote_copy(
            src_ref=ow_part(source, origin),
            dst_ref=ow_part(source, origin),
            send_sem=op_send.at[k, m],
            recv_sem=op_recv.at[k, m],
            device_id=group_peer(m)[0],
            device_id_type=MESH,
        ).wait_recv()

    head_of_lane = lax.broadcasted_iota(jnp.int32, (total, local_width), 1)
    head_masks = [
        jnp.logical_and(head_of_lane >= h * HEAD_DIM, head_of_lane < (h + 1) * HEAD_DIM)
        for h in range(local_heads)
    ]
    scale = 1.0 / math.sqrt(HEAD_DIM)

    def project(s):
        rows = tok[s].reshape(total, width).astype(jnp.float32)
        normed = normalize(rows, token_gain[...]).astype(jnp.bfloat16)
        for index, target in enumerate((query, key, value)):
            target[s] = lax.dot_general(
                normed, qkv[index], (((1,), (1,)), ((), ())), preferred_element_type=jnp.float32
            ).astype(jnp.bfloat16)

    def attend(s):
        keys, values = key[s].astype(jnp.float32), value[s].astype(jnp.float32)
        keys = jnp.concatenate(
            [jnp.where(mask, keys, 0.0).astype(jnp.bfloat16) for mask in head_masks], axis=0
        )
        values = jnp.concatenate(
            [jnp.where(mask, values, 0.0).astype(jnp.bfloat16) for mask in head_masks], axis=0
        )
        scores = lax.dot_general(
            query[s], keys, (((1,), (1,)), ((), ())), preferred_element_type=jnp.float32
        )
        probs = []
        for h in range(local_heads):
            mine = scores[:, h * total : (h + 1) * total] * scale + bias[:, h * total : (h + 1) * total]
            weights = jnp.exp(mine - jnp.max(mine, axis=-1, keepdims=True))
            inverse = 1.0 / jnp.sum(weights, axis=-1, keepdims=True)
            probs.append((weights * inverse).astype(jnp.bfloat16))
        mixed = jnp.dot(
            jnp.concatenate(probs, axis=1), values, preferred_element_type=jnp.float32
        ).astype(jnp.bfloat16)
        attended[s] = mixed.reshape(n_row, token_rows, local_width)

    def att_copy(s, k):
        dest = row_peer(k)
        return pltpu.make_async_remote_copy(
            src_ref=attended.at[s, dest],
            dst_ref=heads_in.at[me, s],
            send_sem=at_send.at[s, k],
            recv_sem=at_recv.at[s, k],
            device_id={"row": dest},
            device_id_type=MESH,
        )

    def att_wait(s, k):
        source = row_peer(n_row - k)
        pltpu.make_async_remote_copy(
            src_ref=heads_in.at[source, s],
            dst_ref=heads_in.at[source, s],
            send_sem=at_send.at[s, k],
            recv_sem=at_recv.at[s, k],
            device_id={"row": row_peer(k)},
            device_id_type=MESH,
        ).wait_recv()

    def give(s):
        for k in range(1, n_row):
            att_copy(s, k).start()
        heads_in[me, s] = attended[s, me]

    loads["ow"].wait()
    for s in range(samples):
        pass_on(1, s)
    for k in range(1, n_row):
        ow_row_copy(k).start()
    def spread_bias():
        for k in range(1, n_row):
            bias_row_wait(k)
            for m in range(1, n_plane):
                bias_plane_copy(k, m).start()

    for k in range(2, n_row - 1):
        for s in range(samples):
            if k == 2 and s == 1:
                spread_bias()
            pass_on(k, s)
    if n_row < 4 or samples < 2:
        spread_bias()
    if shared:
        for k in range(1, n_row):
            ow_row_wait(k)
            for m in range(1, pieces):
                ow_group_copy(k, m).start()
    for name in ("token_gain", "qkv"):
        loads[name].wait()

    own_bias.wait()
    for k in range(n_row):
        for m in range(1, n_plane):
            bias_plane_wait(k, m)
    lanes_at = lax.broadcasted_iota(jnp.int32, (head_rows, LANES), 1)
    for tile in range(total // LANES):
        padded = lanes_at[:stripes] + tile * LANES >= valid[0]
        for r in range(n_row):
            parts = [bias_recv[r, tile * fold + m] for m in range(fold)]
            for q in range(fold):
                whole = None
                for m in range(fold):
                    shift = ((m - q) % fold) * tile_cols
                    turned = pltpu.roll(parts[m], shift, 1) if shift else parts[m]
                    whole = (
                        turned
                        if whole is None
                        else jnp.where(lanes_at >= m * tile_cols, turned, whole)
                    )
                at = r * tile_rows + q * stripes
                for h in range(local_heads):
                    bias[
                        at : at + stripes,
                        h * total + tile * LANES : h * total + (tile + 1) * LANES,
                    ] = jnp.where(padded, -1e30, whole[h * stripes : (h + 1) * stripes])

    for s in range(samples):
        if n_row > 2:
            pass_on(n_row - 1, s)
        project(s)
        attend(s)
        give(s)

    for k in range(1, n_row):
        if shared:
            for m in range(1, pieces):
                ow_group_wait(k, m)
        else:
            ow_row_wait(k)

    def update_of(source):
        flat = heads_in[source].reshape(samples * token_rows, local_width)
        return jnp.dot(flat, ow[source], preferred_element_type=jnp.float32)

    update = tok[:, me].reshape(samples * token_rows, width).astype(jnp.float32) + 0.0
    product = update_of(me)
    for k in range(1, n_row):
        for s in range(samples):
            att_wait(s, k)
        product = product + update_of(row_peer(n_row - k))
    out[...] = (update + product).astype(out.dtype).reshape(samples, token_rows, width)

    for s in range(samples):
        finish_tok_sends(s)
        for k in range(1, n_row):
            att_copy(s, k).wait_send()
    for k in range(1, n_row):
        bias_row_copy(k).wait_send()
        ow_row_copy(k).wait_send()
        if shared:
            for m in range(1, pieces):
                ow_group_copy(k, m).wait_send()
    for k in range(n_row):
        for m in range(1, n_plane):
            bias_plane_copy(k, m).wait_send()


def per_device(
    axes,
    pair_repr,
    asym_id,
    valid_len,
    rel_embed,
    pair_gain,
    bias_weight,
    tokens,
    token_gain,
    qkv_weight,
    out_weight,
):
    n_job, n_row, n_col, n_samp = axes
    samples, token_rows, width = tokens.shape
    total = n_row * token_rows
    n_plane = n_col * n_samp
    heads = bias_weight.shape[1]
    local_heads = heads // n_row
    tile_rows, tile_cols, channels = pair_repr.shape
    local_width = qkv_weight.shape[-1]
    out_rows = out_weight.shape[1]
    row_pieces = 1 if out_rows % (16 * n_job * n_samp) else n_job * n_samp
    col_pieces = 1 if width % (LANES * n_col) else n_col
    pieces = row_pieces * col_pieces
    stripes = tile_rows // (LANES // tile_cols)
    head_rows = local_heads * stripes
    bf16, f32 = jnp.bfloat16, jnp.float32
    dma = pltpu.SemaphoreType.DMA
    any_spec = pl.BlockSpec(memory_space=pl.ANY)
    return pl.pallas_call(
        functools.partial(kernel, axes, (row_pieces, col_pieces)),
        out_shape=jax.ShapeDtypeStruct(tokens.shape, tokens.dtype),
        in_specs=[any_spec] * 10,
        out_specs=pl.BlockSpec(memory_space=pltpu.VMEM),
        scratch_shapes=[
            pltpu.SMEM(asym_id.shape, jnp.int32),
            pltpu.SMEM(valid_len.shape, jnp.int32),
            pltpu.VMEM(pair_repr.shape, bf16),
            pltpu.VMEM(rel_embed.shape, bf16),
            pltpu.VMEM((1, channels), f32),
            pltpu.VMEM(bias_weight.shape[::-1], bf16),
            pltpu.VMEM(token_gain.shape, f32),
            pltpu.VMEM((3, local_width, width), bf16),
            pltpu.VMEM((samples, n_row, token_rows, width), bf16),
            pltpu.VMEM((n_row, out_rows, width), bf16),
            pltpu.VMEM((heads * stripes, LANES), f32),
            pltpu.VMEM((n_row, n_plane, head_rows, LANES), f32),
            pltpu.VMEM((total, local_heads * total), f32),
            pltpu.VMEM((samples, total, local_width), bf16),
            pltpu.VMEM((samples, total, local_width), bf16),
            pltpu.VMEM((samples, total, local_width), bf16),
            pltpu.VMEM((samples, n_row, token_rows, local_width), bf16),
            pltpu.VMEM((n_row, samples, token_rows, local_width), bf16),
            dma((9,)),
            dma((samples,)),
            dma((2, samples, n_row)),
            dma((samples, n_row)),
            dma((n_row,)),
            dma((n_row,)),
            dma((n_row, n_plane)),
            dma((n_row, n_plane)),
            dma,
            dma((n_row,)),
            dma((n_row,)),
            dma((n_row, pieces)),
            dma((n_row, pieces)),
            dma((samples, n_row)),
            dma((samples, n_row)),
        ],
        compiler_params=pltpu.CompilerParams(
            collective_id=0, has_side_effects=True, vmem_limit_bytes=60 * 1024 * 1024
        ),
    )(
        asym_id,
        valid_len,
        pair_repr,
        rel_embed,
        pair_gain.reshape(1, channels),
        bias_weight.T,
        tokens,
        token_gain,
        jnp.swapaxes(qkv_weight, 2, 3),
        out_weight,
    )


def solution(mesh):
    axes = tuple(mesh.shape[name] for name in ("job", "row", "col", "samp"))
    return jax.shard_map(
        functools.partial(per_device, axes),
        mesh=mesh,
        in_specs=(
            P(("job", "row"), ("col", "samp"), None),
            P("job"),
            P("job"),
            P(),
            P(),
            P(),
            P(("job", "col", "samp"), "row", None),
            P(),
            P(None, None, None, "row"),
            P(None, "row", None),
        ),
        out_specs=P(("job", "col", "samp"), "row", None),
        check_vma=False,
    )
```

profile of v0, /device:TPU:1, one launch (start us, length us, event | category | flops | bytes accessed | tf_op | source)
XLA Modules:
  0.0 33.5 jit_solution(16604136826227921319)
XLA Ops:
  0.7 31.3 %shard_map.100 = bf16[4,32,768]{2,1,0:T(8,128)(2,1)} custom-call(s32[128]{0:T(128)} %asym_hbm.1, s32[1]{0:T(128)S(6)} %copy.12.valid_hbm, bf16[32,32,128]{2,1,0:T(8,128)(2,1)} %pair_hbm.1, bf16[128,128]{1,0:T(8,128)(2,1)} %rel_hbm.1, f32[1,128]{1,0:T(1,128)} %bitcast.5, bf16[16,128]{1,0:T(8,128)(2,1)} %bitcast.4, bf16[4,32,768]{2,1,0:T(8,128)(2,1)} %tokens_hbm.1, ...), custom_call_target="tpu_custom_call" | custom-call | tf_op jit(solution)/shard_map/pallas_call | solution.py:526
  31.9 1.6 %copy.13 = bf16[4,32,768]{2,1,0:T(8,128)(2,1)} copy(bf16[4,32,768]{2,1,0:T(8,128)(2,1)} %shard_map.100) | data formatting | bytes 393216
where the time goes:
time: 34.2 us; the launch traced here: 33.5 us
  Pallas kernels  31.3 us (92%)
  local copies, waits for them, and re-layouts  1.62 us (5%)
  between operations  0.66 us (2%)
    pallas_call x1, Pallas kernels, per_device(): pl.pallas_call(functools.partial(kernel, axes, (row_pieces, col_pieces)),...  31.3 us
    unnamed x1, local copies, waits for them, and re-layouts  1.62 us

commit v1 on v0

v1 whole, which is shorter than its diff:
```python
import contextlib
import functools
import math

import jax
import jax.numpy as jnp
from jax import lax
from jax.experimental import pallas as pl
from jax.experimental.pallas import tpu as pltpu
from jax.sharding import PartitionSpec as P

HEAD_DIM = 48
EPSILON = 1e-05
LANES = 128
MESH = pl.DeviceIdType.MESH
mark = contextlib.nullcontext


def normalize(values, gain_vector):
    average = jnp.mean(values, axis=-1, keepdims=True)
    centered = values - average
    variance = jnp.mean(centered * centered, axis=-1, keepdims=True)
    return centered * lax.rsqrt(variance + EPSILON) * gain_vector


def back(position, shift, size):
    return lax.rem(position + (size - shift), size) if shift else position


def aligned(value, unit):
    return value if isinstance(value, int) else pl.multiple_of(value, unit)


def kernel(
    axes,
    cuts,
    asym_hbm,
    valid_hbm,
    pair_hbm,
    rel_hbm,
    pair_gain_hbm,
    bias_weight_hbm,
    tokens_hbm,
    token_gain_hbm,
    qkv_hbm,
    out_weight_hbm,
    out,
    asym,
    valid,
    pair,
    rel,
    pair_gain,
    bias_weight,
    token_gain,
    qkv,
    tok,
    ow,
    bias_send,
    bias_recv,
    bias,
    query,
    key,
    value,
    attended,
    heads_in,
    local_sem,
    tok_got,
    tok_sent,
    bias_got,
    ow_got,
    att_got,
    sent,
):
    n_job, n_row, n_col, n_samp = axes
    job, me = lax.axis_index("job"), lax.axis_index("row")
    col, samp = lax.axis_index("col"), lax.axis_index("samp")
    samples, token_rows, width = tokens_hbm.shape
    total = n_row * token_rows
    tile_rows, tile_cols, channels = pair.shape
    bins = rel.shape[0]
    plane = col * n_samp + samp
    all_heads = bias_weight.shape[0]
    local_heads = all_heads // n_row
    local_width = local_heads * HEAD_DIM
    fold = LANES // tile_cols
    stripes = tile_rows // fold
    part_rows = bias_recv.shape[1]
    out_rows = ow.shape[1]
    n_plane = n_col * n_samp
    p_job, p_col, p_samp = cuts
    pieces = p_job * p_col * p_samp
    piece_rows, piece_cols = out_rows // (p_job * p_samp), width // p_col
    here = (job if p_job > 1 else 0, col if p_col > 1 else 0, samp if p_samp > 1 else 0)

    def row_peer(k):
        return lax.rem(me + k, n_row)

    def row_source(k):
        return back(me, k, n_row)

    def send(source, target, left, got, device):
        pltpu.make_async_remote_copy(
            src_ref=source,
            dst_ref=target,
            send_sem=left,
            recv_sem=got,
            device_id=device,
            device_id_type=MESH,
        ).start()

    def awaiting(ref, semaphore):
        return pltpu.make_async_remote_copy(
            src_ref=ref,
            dst_ref=ref,
            send_sem=semaphore,
            recv_sem=semaphore,
            device_id={"row": row_peer(1)},
            device_id_type=MESH,
        )

    def arrive(ref, semaphore):
        awaiting(ref, semaphore).wait_recv()

    barrier = pltpu.get_barrier_semaphore()
    greeted = 0
    for k in range(1, n_row):
        pl.semaphore_signal(barrier, inc=1, device_id={"row": row_peer(k)}, device_id_type=MESH)
        greeted += 1
    for a in range(p_job):
        for b in range(n_col):
            for c in range(n_samp):
                device = {
                    name: lax.rem(spot + step, size)
                    for name, spot, step, size in zip(
                        ("job", "col", "samp"), (job, col, samp), (a, b, c), (n_job, n_col, n_samp)
                    )
                    if step
                }
                if device:
                    pl.semaphore_signal(barrier, inc=1, device_id=device, device_id_type=MESH)
                    greeted += 1

    loads = {}
    for index, (name, source, target) in enumerate(
        (
            ("asym", asym_hbm, asym),
            ("pair", pair_hbm, pair),
            ("rel", rel_hbm, rel),
            ("pair_gain", pair_gain_hbm, pair_gain),
            ("bias_weight", bias_weight_hbm, bias_weight),
            ("qkv", qkv_hbm.at[0], qkv),
            ("token_gain", token_gain_hbm, token_gain),
            ("ow", out_weight_hbm.at[0], ow.at[me]),
            ("valid", valid_hbm, valid),
        )
    ):
        loads[name] = pltpu.make_async_copy(source, target, local_sem.at[index])
    loads["tok"] = pltpu.make_async_copy(tokens_hbm, tok.at[:, me], local_sem.at[9])
    for name in ("asym", "pair", "rel", "pair_gain", "bias_weight", "tok", "qkv", "token_gain", "ow", "valid"):
        loads[name].start()

    with mark("pairload"):
        for name in ("asym", "pair", "rel", "pair_gain", "bias_weight"):
            loads[name].wait()
    first_row, first_col = me * tile_rows, plane * tile_cols
    sub = lax.broadcasted_iota(jnp.int32, (tile_cols, LANES), 0)
    lane = lax.broadcasted_iota(jnp.int32, (tile_cols, LANES), 1)
    with mark("pair"):
        col_chain = jnp.zeros((tile_cols, LANES), jnp.int32)
        for j in range(tile_cols):
            col_chain = jnp.where(sub == j, asym[first_col + j], col_chain)
        reach = bins // 2 - 1
        turned_weight = bias_weight[...]
        for t in range(stripes):
            hots, rows = [], []
            for q in range(fold):
                i = q * stripes + t
                offset = jnp.clip(first_row + i - first_col - sub, -reach, reach) + reach
                bin_ids = jnp.where(col_chain == asym[first_row + i], offset, bins - 1)
                hots.append(jnp.where(bin_ids == lane, 1.0, 0.0).astype(jnp.bfloat16))
                rows.append(pair[i].astype(jnp.float32))
            summed = jnp.concatenate(rows, axis=0) + jnp.dot(
                jnp.concatenate(hots, axis=0), rel[...], preferred_element_type=jnp.float32
            )
            normed_pair = normalize(summed, pair_gain[...]).astype(jnp.bfloat16)
            projected = lax.dot_general(
                turned_weight, normed_pair, (((1,), (1,)), ((), ())), preferred_element_type=jnp.float32
            )
            bias_send[pl.ds(t, all_heads, stride=stripes), :] = projected

    with mark("loads"):
        for name in ("tok", "ow", "qkv", "token_gain", "valid"):
            loads[name].wait()
    with mark("barrier"):
        pl.semaphore_wait(barrier, greeted)

    def ow_piece(source):
        first = aligned((here[0] * p_samp + here[2]) * piece_rows, piece_rows)
        start = aligned(here[1] * piece_cols, piece_cols)
        return ow.at[source, pl.ds(first, piece_rows), pl.ds(start, piece_cols)]

    def send_ow():
        for k in range(1, n_row):
            send(ow_piece(me), ow_piece(me), sent.at[2], ow_got.at[0, k - 1], {"row": row_peer(k)})

    shifts = [
        (a, b, c) for a in range(p_job) for b in range(p_col) for c in range(p_samp) if a or b or c
    ]

    def spread_ow(k):
        piece = ow_piece(row_source(k))
        arrive(piece, ow_got.at[0, k - 1])
        for shift in shifts:
            device = {
                name: lax.rem(spot + step, size)
                for name, spot, step, size in zip(("job", "col", "samp"), here, shift, cuts)
                if step
            }
            send(piece, piece, sent.at[2], ow_got.at[1, k - 1], device)

    def take_ow(k):
        if pieces > 1:
            arrive(ow.at[row_source(k), pl.ds(0, out_rows - out_rows // pieces)], ow_got.at[1, k - 1])

    has_right, has_left = me < n_row - 1, me > 0
    edge = jnp.logical_or(me == 0, me == n_row - 1)
    def push_tokens(s, source, rightward):
        send(
            tok.at[s, source],
            tok.at[s, source],
            tok_sent.at[0 if rightward else 1, source],
            tok_got.at[s, source],
            {"row": jnp.minimum(me + 1, n_row - 1) if rightward else jnp.maximum(me - 1, 0)},
        )

    def send_tokens(s):
        @pl.when(has_right)
        def _():
            push_tokens(s, me, True)

        @pl.when(has_left)
        def _():
            push_tokens(s, me, False)

    def take_tokens(s, distance):
        @pl.when(me >= distance)
        def _():
            source = jnp.maximum(me - distance, 0)
            arrive(tok.at[s, source], tok_got.at[s, source])

            @pl.when(has_right)
            def _():
                push_tokens(s, source, True)

        @pl.when(me + distance < n_row)
        def _():
            source = jnp.minimum(me + distance, n_row - 1)
            arrive(tok.at[s, source], tok_got.at[s, source])

            @pl.when(has_left)
            def _():
                push_tokens(s, source, False)

    def bias_part(target):
        return bias_send.at[
            pl.ds(pl.multiple_of(target * part_rows, part_rows), part_rows)
        ]

    def spread_bias(k):
        place = bias_recv.at[row_source(k) * n_plane + plane]
        held = place if k else bias_part(me)
        for m in range(1, n_plane):
            other = lax.rem(plane + m, n_plane)
            send(
                held,
                place,
                sent.at[1],
                bias_got.at[n_row - 1],
                {"col": lax.div(other, n_samp), "samp": lax.rem(other, n_samp)},
            )

    def send_bias():
        for k in range(1, n_row):
            target = row_peer(k)
            send(
                bias_part(target),
                bias_recv.at[me * n_plane + plane],
                sent.at[1],
                bias_got.at[k - 1],
                {"row": target},
            )
        spread_bias(0)

    def pass_bias(k):
        arrive(bias_recv.at[row_source(k) * n_plane + plane], bias_got.at[k - 1])
        spread_bias(k)

    def take_bias():
        if n_plane > 1:
            arrive(bias_recv.at[pl.ds(0, n_row * (n_plane - 1))], bias_got.at[n_row - 1])

    own_bias = pltpu.make_async_copy(
        bias_part(me), bias_recv.at[me * n_plane + plane], local_sem.at[11]
    )

    head_of_lane = lax.broadcasted_iota(jnp.int32, (total, local_width), 1)
    head_masks = [
        jnp.logical_and(head_of_lane >= h * HEAD_DIM, head_of_lane < (h + 1) * HEAD_DIM)
        for h in range(local_heads)
    ]
    scale = 1.0 / math.sqrt(HEAD_DIM)

    def project(sources, chosen=slice(None)):
        rows = tok[chosen, sources].reshape(-1, width).astype(jnp.float32)
        normed = normalize(rows, token_gain[...]).astype(jnp.bfloat16)
        for index, target in enumerate((query, key, value)):
            done = lax.dot_general(
                normed, qkv[index], (((1,), (1,)), ((), ())), preferred_element_type=jnp.float32
            ).astype(jnp.bfloat16)
            target[chosen, sources] = done.reshape(target[chosen, sources].shape)

    def attend(s):
        whole = (total, local_width)
        keys = key[s].reshape(whole).astype(jnp.float32)
        values = value[s].reshape(whole).astype(jnp.float32)
        keys = jnp.concatenate(
            [jnp.where(mask, keys, 0.0).astype(jnp.bfloat16) for mask in head_masks], axis=0
        )
        values = jnp.concatenate(
            [jnp.where(mask, values, 0.0).astype(jnp.bfloat16) for mask in head_masks], axis=0
        )
        scores = lax.dot_general(
            query[s].reshape(whole), keys, (((1,), (1,)), ((), ())), preferred_element_type=jnp.float32
        )
        probs = []
        for h in range(local_heads):
            span = slice(h * total, (h + 1) * total)
            logits = scores[:, span] * scale + bias[:, span]
            weights = jnp.exp(logits - jnp.max(logits, axis=-1, keepdims=True))
            inverse = 1.0 / jnp.sum(weights, axis=-1, keepdims=True)
            probs.append((weights * inverse).astype(jnp.bfloat16))
        mixed = jnp.dot(
            jnp.concatenate(probs, axis=1), values, preferred_element_type=jnp.float32
        ).astype(jnp.bfloat16)
        attended[s] = mixed.reshape(n_row, token_rows, local_width)

    def give(s):
        for d in range(1, n_row):
            target = row_peer(d)
            send(attended.at[s, target], heads_in.at[me * samples + s], sent.at[0], att_got.at[0], {"row": target})
        heads_in[me * samples + s] = attended[s, me]

    def take_attended():
        arrive(heads_in.at[pl.ds(0, (n_row - 1) * samples)], att_got.at[0])

    def build_bias():
        lanes_at = lax.broadcasted_iota(jnp.int32, (part_rows, LANES), 1)
        for tile in range(total // LANES):
            padded = lanes_at[:stripes] + tile * LANES >= valid[0]
            for r in range(n_row):
                parts = [bias_recv[r * n_plane + tile * fold + m] for m in range(fold)]
                for q in range(fold):
                    whole = None
                    for m in range(fold):
                        shift = ((m - q) % fold) * tile_cols
                        turned = pltpu.roll(parts[m], shift, 1) if shift else parts[m]
                        whole = (
                            turned
                            if whole is None
                            else jnp.where(lanes_at >= m * tile_cols, turned, whole)
                        )
                    at = r * tile_rows + q * stripes
                    for h in range(local_heads):
                        bias[
                            at : at + stripes,
                            h * total + tile * LANES : h * total + (tile + 1) * LANES,
                        ] = jnp.where(padded, -1e30, whole[h * stripes : (h + 1) * stripes])

    everything = slice(None)
    send_bias()
    send_ow()
    own_bias.start()
    for s in range(samples):
        send_tokens(s)

    @pl.when(edge)
    def _():
        with mark("project"):
            project(me)

    with mark("bias0"):
        for k in range(1, n_row):
            pass_bias(k)
    with mark("ow0"):
        for k in range(1, n_row):
            spread_ow(k)
    for distance in range(1, n_row - 1):
        with mark("tokens"):
            for s in range(samples):
                take_tokens(s, distance)

        @pl.when(edge)
        def _():
            with mark("project"):
                project(jnp.where(me == 0, distance, me - distance))

    def prepare_bias():
        with mark("bias2"):
            own_bias.wait()
            take_bias()
        with mark("build"):
            build_bias()

    def finish_sample(s):
        with mark("attend"):
            attend(s)
        with mark("give"):
            give(s)

    @pl.when(edge)
    def _():
        prepare_bias()
        for s in range(samples):
            with mark("tokense"):
                take_tokens(s, n_row - 1)
            with mark("project"):
                project(n_row - 1 - me, slice(s, s + 1))
            finish_sample(s)

    @pl.when(jnp.logical_not(edge))
    def _():
        for s in range(samples):
            with mark("tokensi"):
                take_tokens(s, n_row - 1)
        with mark("projecti"):
            project(slice(None))
        prepare_bias()
        for s in range(samples):
            finish_sample(s)

    with mark("ow3"):
        for k in range(1, n_row):
            take_ow(k)
    with mark("attwait"):
        take_attended()

    with mark("product"):
        result = tok[:, me].reshape(samples * token_rows, width).astype(jnp.float32)
        product = None
        for r in range(n_row):
            flat = heads_in[r * samples : (r + 1) * samples].reshape(samples * token_rows, local_width)
            term = jnp.dot(flat, ow[r], preferred_element_type=jnp.float32)
            product = term if product is None else product + term
        out[...] = (result + product).astype(out.dtype).reshape(samples, token_rows, width)

    with mark("fin"):
        for source in range(n_row):
            for rightward in (True, False):

                @pl.when(jnp.logical_and(source <= me, has_right) if rightward else jnp.logical_and(source >= me, has_left))
                def _():
                    awaiting(tok.at[:, source], tok_sent.at[0 if rightward else 1, source]).wait_send()

        awaiting(bias_recv.at[pl.ds(0, n_row * n_plane - 1)], sent.at[1]).wait_send()
        awaiting(attended.at[:, pl.ds(0, n_row - 1)], sent.at[0]).wait_send()
        awaiting(ow.at[pl.ds(0, n_row - 1)], sent.at[2]).wait_send()


def per_device(
    axes,
    pair_repr,
    asym_id,
    valid_len,
    rel_embed,
    pair_gain,
    bias_weight,
    tokens,
    token_gain,
    qkv_weight,
    out_weight,
):
    n_job, n_row, n_col, n_samp = axes
    samples, token_rows, width = tokens.shape
    total = n_row * token_rows
    n_plane = n_col * n_samp
    heads = bias_weight.shape[1]
    local_heads = heads // n_row
    tile_rows, tile_cols, channels = pair_repr.shape
    local_width = qkv_weight.shape[-1]
    out_rows = out_weight.shape[1]
    cut_rows = out_rows % (16 * n_job * n_samp) == 0
    cut_cols = width % (LANES * n_col) == 0
    cuts = (n_job if cut_rows else 1, n_col if cut_cols else 1, n_samp if cut_rows else 1)
    stripes = tile_rows // (LANES // tile_cols)
    part_rows = local_heads * stripes
    bf16, f32 = jnp.bfloat16, jnp.float32
    dma = pltpu.SemaphoreType.DMA
    any_spec = pl.BlockSpec(memory_space=pltpu.HBM)
    return pl.pallas_call(
        functools.partial(kernel, axes, cuts),
        out_shape=jax.ShapeDtypeStruct(tokens.shape, tokens.dtype),
        in_specs=[any_spec] * 10,
        out_specs=pl.BlockSpec(memory_space=pltpu.VMEM),
        scratch_shapes=[
            pltpu.SMEM(asym_id.shape, jnp.int32),
            pltpu.SMEM(valid_len.shape, jnp.int32),
            pltpu.VMEM(pair_repr.shape, bf16),
            pltpu.VMEM(rel_embed.shape, bf16),
            pltpu.VMEM((1, channels), f32),
            pltpu.VMEM(bias_weight.shape[::-1], bf16),
            pltpu.VMEM(token_gain.shape, f32),
            pltpu.VMEM((3, local_width, width), bf16),
            pltpu.VMEM((samples, n_row, token_rows, width), bf16),
            pltpu.VMEM((n_row, out_rows, width), bf16),
            pltpu.VMEM((heads * stripes, LANES), f32),
            pltpu.VMEM((n_row * n_plane, part_rows, LANES), f32),
            pltpu.VMEM((total, local_heads * total), f32),
            pltpu.VMEM((samples, n_row, token_rows, local_width), bf16),
            pltpu.VMEM((samples, n_row, token_rows, local_width), bf16),
            pltpu.VMEM((samples, n_row, token_rows, local_width), bf16),
            pltpu.VMEM((samples, n_row, token_rows, local_width), bf16),
            pltpu.VMEM((n_row * samples, token_rows, local_width), bf16),
            dma((12,)),
            dma((samples, n_row)),
            dma((2, n_row)),
            dma((n_row,)),
            dma((2, n_row - 1)),
            dma((1,)),
            dma((3,)),
        ],
        compiler_params=pltpu.CompilerParams(
            collective_id=0, has_side_effects=True, vmem_limit_bytes=24 * 1024 * 1024
        ),
    )(
        *(
            operand if operand is valid_len else pltpu.with_memory_space_constraint(operand, pltpu.HBM)
            for operand in (
                asym_id,
                valid_len,
                pair_repr,
                rel_embed,
                pair_gain.reshape(1, channels),
                bias_weight.T,
                tokens,
                token_gain,
                jnp.swapaxes(qkv_weight, 2, 3),
                out_weight,
            )
        )
    )


def solution(mesh):
    axes = tuple(mesh.shape[name] for name in ("job", "row", "col", "samp"))
    return jax.shard_map(
        functools.partial(per_device, axes),
        mesh=mesh,
        in_specs=(
            P(("job", "row"), ("col", "samp"), None),
            P("job"),
            P("job"),
            P(),
            P(),
            P(),
            P(("job", "col", "samp"), "row", None),
            P(),
            P(None, None, None, "row"),
            P(None, "row", None),
        ),
        out_specs=P(("job", "col", "samp"), "row", None),
        check_vma=False,
    )
```

time: 34.2 us -> 31.2 us (0.912)
  the two profiles are of different devices: /device:TPU:1 before, /device:TPU:0 now
where the time goes in v1:
time: 31.2 us; the launch traced here: 31 us
  Pallas kernels  29.7 us (95%)
  local copies, waits for them, and re-layouts  0.68 us (2%)
  between operations  0.66 us (2%)
    pallas_call x1, Pallas kernels, per_device(): pl.pallas_call(functools.partial(kernel, axes, cuts), out_shape=jax.Shape...  29.7 us
    unnamed x1, local copies, waits for them, and re-layouts  0.68 us

profile of v1, /device:TPU:0, one launch (start us, length us, event | category | flops | bytes accessed | tf_op | source)
XLA Modules:
  0.0 31.0 jit_solution(11169165550433530791)
XLA Ops:
  0.7 29.7 %shard_map.100 = bf16[4,32,768]{2,1,0:T(8,128)(2,1)S(1)} custom-call(s32[128]{0:T(128)} %asym_hbm.1, s32[1]{0:T(128)S(6)} %copy.12.valid_hbm, bf16[32,32,128]{2,1,0:T(8,128)(2,1)} %pair_hbm.1, bf16[128,128]{1,0:T(8,128)(2,1)} %rel_hbm.1, f32[1,128]{1,0:T(1,128)} %bitcast.5, bf16[16,128]{1,0:T(8,128)(2,1)} %bitcast.4, bf16[4,32,768]{2,1,0:T(8,128)(2,1)} %tokens_hbm.1, ...), custom_call_target="tpu_custom_call" | custom-call | tf_op jit(solution)/shard_map/pallas_call | solution.py:499
  30.3 0.7 %copy.13 = bf16[4,32,768]{2,1,0:T(8,128)(2,1)} copy(bf16[4,32,768]{2,1,0:T(8,128)(2,1)S(1)} %shard_map.100) | data formatting | bytes 393216

commit v2 on v1

--- a/solution.py
+++ b/solution.py
@@ -68,8 +68,10 @@
     tok_sent,
     bias_got,
     ow_got,
+    ow_sent,
     att_got,
     sent,
+    greeting,
 ):
     n_job, n_row, n_col, n_samp = axes
     job, me = lax.axis_index("job"), lax.axis_index("row")
@@ -87,10 +89,10 @@
     part_rows = bias_recv.shape[1]
     out_rows = ow.shape[1]
     n_plane = n_col * n_samp
-    p_job, p_col, p_samp = cuts
-    pieces = p_job * p_col * p_samp
-    piece_rows, piece_cols = out_rows // (p_job * p_samp), width // p_col
-    here = (job if p_job > 1 else 0, col if p_col > 1 else 0, samp if p_samp > 1 else 0)
+    p_job, p_col = cuts
+    pieces = p_job * p_col
+    piece_rows, piece_cols = out_rows // p_job, width // p_col
+    relay = samp == n_samp - 1
 
     def row_peer(k):
         return lax.rem(me + k, n_row)
@@ -121,24 +123,32 @@
     def arrive(ref, semaphore):
         awaiting(ref, semaphore).wait_recv()
 
+    has_right, has_left = me < n_row - 1, me > 0
+    edge = jnp.logical_or(me == 0, me == n_row - 1)
+
+    def greet(semaphore):
+        for name, spot, size in (("col", col, n_col), ("samp", samp, n_samp), ("job", job, p_job)):
+            for k in range(1, size):
+                device = {name: lax.rem(spot + k, size)}
+                pl.semaphore_signal(semaphore, inc=1, device_id=device, device_id_type=MESH)
+
+        @pl.when(has_right)
+        def _():
+            device = {"row": jnp.minimum(me + 1, n_row - 1)}
+            pl.semaphore_signal(semaphore, inc=1, device_id=device, device_id_type=MESH)
+
+        @pl.when(has_left)
+        def _():
+            device = {"row": jnp.maximum(me - 1, 0)}
+            pl.semaphore_signal(semaphore, inc=1, device_id=device, device_id_type=MESH)
+
+    def await_greetings(semaphore):
+        others = (n_col - 1) + (n_samp - 1) + (p_job - 1)
+        pl.semaphore_wait(semaphore, others + jnp.where(edge, 1, 2))
+
+    rounds = greeting.shape[0]
     barrier = pltpu.get_barrier_semaphore()
-    greeted = 0
-    for k in range(1, n_row):
-        pl.semaphore_signal(barrier, inc=1, device_id={"row": row_peer(k)}, device_id_type=MESH)
-        greeted += 1
-    for a in range(p_job):
-        for b in range(n_col):
-            for c in range(n_samp):
-                device = {
-                    name: lax.rem(spot + step, size)
-                    for name, spot, step, size in zip(
-                        ("job", "col", "samp"), (job, col, samp), (a, b, c), (n_job, n_col, n_samp)
-                    )
-                    if step
-                }
-                if device:
-                    pl.semaphore_signal(barrier, inc=1, device_id=device, device_id_type=MESH)
-                    greeted += 1
+    greet(barrier)
 
     loads = {}
     for index, (name, source, target) in enumerate(
@@ -156,74 +166,47 @@
     ):
         loads[name] = pltpu.make_async_copy(source, target, local_sem.at[index])
     loads["tok"] = pltpu.make_async_copy(tokens_hbm, tok.at[:, me], local_sem.at[9])
-    for name in ("asym", "pair", "rel", "pair_gain", "bias_weight", "tok", "qkv", "token_gain", "ow", "valid"):
+    for name in ("tok", "asym", "pair", "rel", "pair_gain", "bias_weight", "qkv", "token_gain", "ow", "valid"):
         loads[name].start()
 
-    with mark("pairload"):
-        for name in ("asym", "pair", "rel", "pair_gain", "bias_weight"):
-            loads[name].wait()
-    first_row, first_col = me * tile_rows, plane * tile_cols
-    sub = lax.broadcasted_iota(jnp.int32, (tile_cols, LANES), 0)
-    lane = lax.broadcasted_iota(jnp.int32, (tile_cols, LANES), 1)
-    with mark("pair"):
-        col_chain = jnp.zeros((tile_cols, LANES), jnp.int32)
-        for j in range(tile_cols):
-            col_chain = jnp.where(sub == j, asym[first_col + j], col_chain)
-        reach = bins // 2 - 1
-        turned_weight = bias_weight[...]
-        for t in range(stripes):
-            hots, rows = [], []
-            for q in range(fold):
-                i = q * stripes + t
-                offset = jnp.clip(first_row + i - first_col - sub, -reach, reach) + reach
-                bin_ids = jnp.where(col_chain == asym[first_row + i], offset, bins - 1)
-                hots.append(jnp.where(bin_ids == lane, 1.0, 0.0).astype(jnp.bfloat16))
-                rows.append(pair[i].astype(jnp.float32))
-            summed = jnp.concatenate(rows, axis=0) + jnp.dot(
-                jnp.concatenate(hots, axis=0), rel[...], preferred_element_type=jnp.float32
-            )
-            normed_pair = normalize(summed, pair_gain[...]).astype(jnp.bfloat16)
-            projected = lax.dot_general(
-                turned_weight, normed_pair, (((1,), (1,)), ((), ())), preferred_element_type=jnp.float32
-            )
-            bias_send[pl.ds(t, all_heads, stride=stripes), :] = projected
-
-    with mark("loads"):
-        for name in ("tok", "ow", "qkv", "token_gain", "valid"):
-            loads[name].wait()
-    with mark("barrier"):
-        pl.semaphore_wait(barrier, greeted)
-
-    def ow_piece(source):
-        first = aligned((here[0] * p_samp + here[2]) * piece_rows, piece_rows)
-        start = aligned(here[1] * piece_cols, piece_cols)
+    def ow_piece(source, a, b):
+        first = aligned(lax.rem(job + a, n_job) * piece_rows if p_job > 1 else 0, piece_rows)
+        start = aligned(lax.rem(col + b, n_col) * piece_cols if p_col > 1 else 0, piece_cols)
         return ow.at[source, pl.ds(first, piece_rows), pl.ds(start, piece_cols)]
+
+    chips = [(a, b) for a in range(p_job) for b in range(p_col)]
 
     def send_ow():
         for k in range(1, n_row):
-            send(ow_piece(me), ow_piece(me), sent.at[2], ow_got.at[0, k - 1], {"row": row_peer(k)})
-
-    shifts = [
-        (a, b, c) for a in range(p_job) for b in range(p_col) for c in range(p_samp) if a or b or c
-    ]
+            send(ow_piece(me, 0, 0), ow_piece(me, 0, 0), sent.at[2], ow_got.at[0, k - 1], {"row": row_peer(k)})
+
+    def pair_ow(k, a, b):
+        piece = ow_piece(row_source(k), a, b)
+        for e in range(1, n_samp):
+            device = {"samp": lax.rem(samp + e, n_samp)}
+            send(piece, piece, ow_sent.at[e - 1], ow_got.at[2, k - 1], device)
 
     def spread_ow(k):
-        piece = ow_piece(row_source(k))
+        piece = ow_piece(row_source(k), 0, 0)
         arrive(piece, ow_got.at[0, k - 1])
-        for shift in shifts:
+        for a, b in chips[1:]:
             device = {
                 name: lax.rem(spot + step, size)
-                for name, spot, step, size in zip(("job", "col", "samp"), here, shift, cuts)
+                for name, spot, step, size in (("job", job, a, n_job), ("col", col, b, n_col))
                 if step
             }
             send(piece, piece, sent.at[2], ow_got.at[1, k - 1], device)
-
-    def take_ow(k):
+        pair_ow(k, 0, 0)
+
+    def collect_ow(k):
         if pieces > 1:
             arrive(ow.at[row_source(k), pl.ds(0, out_rows - out_rows // pieces)], ow_got.at[1, k - 1])
-
-    has_right, has_left = me < n_row - 1, me > 0
-    edge = jnp.logical_or(me == 0, me == n_row - 1)
+            for a, b in chips[1:]:
+                pair_ow(k, a, b)
+
+    def take_ow(k):
+        arrive(ow.at[row_source(k)], ow_got.at[2, k - 1])
+
     def push_tokens(s, source, rightward):
         send(
             tok.at[s, source],
@@ -377,32 +360,116 @@
                         ] = jnp.where(padded, -1e30, whole[h * stripes : (h + 1) * stripes])
 
     everything = slice(None)
+    with mark("tokload"):
+        loads["tok"].wait()
+    with mark("barrier"):
+        await_greetings(barrier)
+
+    early = 2
+    for s in range(early):
+        send_tokens(s)
+
+    @pl.when(jnp.logical_not(relay))
+    def _():
+        for s in range(early, samples):
+            send_tokens(s)
+
+    with mark("pairload"):
+        for name in ("asym", "pair", "rel", "pair_gain", "bias_weight"):
+            loads[name].wait()
+    first_row, first_col = me * tile_rows, plane * tile_cols
+    sub = lax.broadcasted_iota(jnp.int32, (tile_cols, LANES), 0)
+    lane = lax.broadcasted_iota(jnp.int32, (tile_cols, LANES), 1)
+    with mark("pairprep"):
+        col_chain = jnp.zeros((tile_cols, LANES), jnp.int32)
+        for j in range(tile_cols):
+            col_chain = jnp.where(sub == j, asym[first_col + j], col_chain)
+        reach = bins // 2 - 1
+        turned_weight = bias_weight[...]
+    def pair_stripes(first, last):
+        for t in range(first, last):
+            hots, rows = [], []
+            for q in range(fold):
+                i = q * stripes + t
+                offset = jnp.clip(first_row + i - first_col - sub, -reach, reach) + reach
+                bin_ids = jnp.where(col_chain == asym[first_row + i], offset, bins - 1)
+                hots.append(jnp.where(bin_ids == lane, 1.0, 0.0).astype(jnp.bfloat16))
+                rows.append(pair[i].astype(jnp.float32))
+            summed = jnp.concatenate(rows, axis=0) + jnp.dot(
+                jnp.concatenate(hots, axis=0), rel[...], preferred_element_type=jnp.float32
+            )
+            normed_pair = normalize(summed, pair_gain[...]).astype(jnp.bfloat16)
+            projected = lax.dot_general(
+                turned_weight, normed_pair, (((1,), (1,)), ((), ())), preferred_element_type=jnp.float32
+            )
+            bias_send[pl.ds(t, all_heads, stride=stripes), :] = projected
+
+    for r in range(rounds):
+        greet(greeting.at[r])
+        with mark("pair"):
+            pair_stripes(r * stripes // rounds, (r + 1) * stripes // rounds)
+        with mark("greeting"):
+            await_greetings(greeting.at[r])
+
+    with mark("loads"):
+        for name in ("ow", "qkv", "token_gain", "valid"):
+            loads[name].wait()
     send_bias()
-    send_ow()
     own_bias.start()
-    for s in range(samples):
-        send_tokens(s)
+
+    @pl.when(relay)
+    def _():
+        send_ow()
+        for s in range(early, samples):
+            send_tokens(s)
 
     @pl.when(edge)
     def _():
         with mark("project"):
             project(me)
 
-    with mark("bias0"):
-        for k in range(1, n_row):
-            pass_bias(k)
-    with mark("ow0"):
-        for k in range(1, n_row):
-            spread_ow(k)
-    for distance in range(1, n_row - 1):
-        with mark("tokens"):
-            for s in range(samples):
+    def step(distance):
+        for s in range(samples):
+            with mark("tokens"):
                 take_tokens(s, distance)
+            if distance == 1 and s == 1:
+
+                @pl.when(relay)
+                def _():
+                    with mark("ow0"):
+                        for k in range(1, n_row):
+                            spread_ow(k)
 
         @pl.when(edge)
         def _():
             with mark("project"):
                 project(jnp.where(me == 0, distance, me - distance))
+
+    def first_bias():
+        with mark("bias0"):
+            for k in range(1, n_row):
+                pass_bias(k)
+
+    @pl.when(relay)
+    def _():
+        first_bias()
+
+    if n_row > 2:
+        step(1)
+
+    @pl.when(jnp.logical_not(relay))
+    def _():
+        first_bias()
+
+    for distance in range(2, n_row - 1):
+        step(distance)
+
+    def relay_ow():
+        @pl.when(relay)
+        def _():
+            with mark("ow1"):
+                for k in range(1, n_row):
+                    collect_ow(k)
 
     def prepare_bias():
         with mark("bias2"):
@@ -411,21 +478,29 @@
         with mark("build"):
             build_bias()
 
-    def finish_sample(s):
+    def finish_samples(first, last):
         with mark("attend"):
-            attend(s)
+            for s in range(first, last):
+                attend(s)
         with mark("give"):
-            give(s)
+            for s in range(first, last):
+                give(s)
+
+    batch = max(samples // 2, 1)
+    batches = [(first, min(first + batch, samples)) for first in range(0, samples, batch)]
 
     @pl.when(edge)
     def _():
         prepare_bias()
-        for s in range(samples):
+        for first, last in batches:
             with mark("tokense"):
-                take_tokens(s, n_row - 1)
+                for s in range(first, last):
+                    take_tokens(s, n_row - 1)
             with mark("project"):
-                project(n_row - 1 - me, slice(s, s + 1))
-            finish_sample(s)
+                project(n_row - 1 - me, slice(first, last))
+            finish_samples(first, last)
+            if first == 0:
+                relay_ow()
 
     @pl.when(jnp.logical_not(edge))
     def _():
@@ -435,12 +510,16 @@
         with mark("projecti"):
             project(slice(None))
         prepare_bias()
-        for s in range(samples):
-            finish_sample(s)
-
-    with mark("ow3"):
-        for k in range(1, n_row):
-            take_ow(k)
+        for first, last in batches:
+            finish_samples(first, last)
+        relay_ow()
+
+    @pl.when(jnp.logical_not(relay))
+    def _():
+        with mark("ow3"):
+            for k in range(1, n_row):
+                take_ow(k)
+
     with mark("attwait"):
         take_attended()
 
@@ -463,7 +542,12 @@
 
         awaiting(bias_recv.at[pl.ds(0, n_row * n_plane - 1)], sent.at[1]).wait_send()
         awaiting(attended.at[:, pl.ds(0, n_row - 1)], sent.at[0]).wait_send()
-        awaiting(ow.at[pl.ds(0, n_row - 1)], sent.at[2]).wait_send()
+
+        @pl.when(relay)
+        def _():
+            awaiting(ow.at[pl.ds(0, n_row - 1)], sent.at[2]).wait_send()
+            for e in range(1, n_samp):
+                awaiting(ow.at[pl.ds(0, n_row - 1)], ow_sent.at[e - 1]).wait_send()
 
 
 def per_device(
@@ -488,9 +572,7 @@
     tile_rows, tile_cols, channels = pair_repr.shape
     local_width = qkv_weight.shape[-1]
     out_rows = out_weight.shape[1]
-    cut_rows = out_rows % (16 * n_job * n_samp) == 0
-    cut_cols = width % (LANES * n_col) == 0
-    cuts = (n_job if cut_rows else 1, n_col if cut_cols else 1, n_samp if cut_rows else 1)
+    cuts = (1 if out_rows % (16 * n_job) else n_job, 1 if width % (LANES * n_col) else n_col)
     stripes = tile_rows // (LANES // tile_cols)
     part_rows = local_heads * stripes
     bf16, f32 = jnp.bfloat16, jnp.float32
@@ -524,9 +606,11 @@
             dma((samples, n_row)),
             dma((2, n_row)),
             dma((n_row,)),
-            dma((2, n_row - 1)),
+            dma((3, n_row - 1)),
+            dma((max(n_samp - 1, 1),)),
             dma((1,)),
             dma((3,)),
+            pltpu.SemaphoreType.REGULAR((max(n_row - 2, 2),)),
         ],
         compiler_params=pltpu.CompilerParams(
             collective_id=0, has_side_effects=True, vmem_limit_bytes=24 * 1024 * 1024

time: 31.2 us -> 29.3 us (0.939)
  the two profiles are of different devices: /device:TPU:0 before, /device:TPU:1 now
where the time goes in v2:
time: 29.3 us; the launch traced here: 29.1 us
  Pallas kernels  27.8 us (95%)
  local copies, waits for them, and re-layouts  0.68 us (2%)
  between operations  0.66 us (2%)
    pallas_call x1, Pallas kernels, per_device(): pl.pallas_call(functools.partial(kernel, axes, cuts), out_shape=jax.Shape...  27.8 us
    unnamed x1, local copies, waits for them, and re-layouts  0.68 us

profile of v2, /device:TPU:1, one launch (start us, length us, event | category | flops | bytes accessed | tf_op | source)
XLA Modules:
  0.0 29.1 jit_solution(18309848127404777791)
XLA Ops:
  0.7 27.8 %shard_map.100 = bf16[4,32,768]{2,1,0:T(8,128)(2,1)S(1)} custom-call(s32[128]{0:T(128)} %asym_hbm.1, s32[1]{0:T(128)S(6)} %copy.12.valid_hbm, bf16[32,32,128]{2,1,0:T(8,128)(2,1)} %pair_hbm.1, bf16[128,128]{1,0:T(8,128)(2,1)} %rel_hbm.1, f32[1,128]{1,0:T(1,128)} %bitcast.5, bf16[16,128]{1,0:T(8,128)(2,1)} %bitcast.4, bf16[4,32,768]{2,1,0:T(8,128)(2,1)} %tokens_hbm.1, ...), custom_call_target="tpu_custom_call" | custom-call | tf_op jit(solution)/shard_map/pallas_call | solution.py:581
  28.4 0.7 %copy.13 = bf16[4,32,768]{2,1,0:T(8,128)(2,1)} copy(bf16[4,32,768]{2,1,0:T(8,128)(2,1)S(1)} %shard_map.100) | data formatting | bytes 393216

commit v3 on v2

--- a/solution.py
+++ b/solution.py
@@ -53,6 +53,7 @@
     bias_weight,
     token_gain,
     qkv,
+    own,
     tok,
     ow,
     bias_send,
@@ -63,6 +64,7 @@
     value,
     attended,
     heads_in,
+    total_sum,
     local_sem,
     tok_got,
     tok_sent,
@@ -165,8 +167,8 @@
         )
     ):
         loads[name] = pltpu.make_async_copy(source, target, local_sem.at[index])
-    loads["tok"] = pltpu.make_async_copy(tokens_hbm, tok.at[:, me], local_sem.at[9])
-    for name in ("tok", "asym", "pair", "rel", "pair_gain", "bias_weight", "qkv", "token_gain", "ow", "valid"):
+    loads["tok"] = pltpu.make_async_copy(tokens_hbm, own, local_sem.at[9])
+    for name in ("tok", "token_gain", "asym", "pair", "rel", "pair_gain", "bias_weight", "qkv", "ow", "valid"):
         loads[name].start()
 
     def ow_piece(source, a, b):
@@ -207,42 +209,42 @@
     def take_ow(k):
         arrive(ow.at[row_source(k)], ow_got.at[2, k - 1])
 
-    def push_tokens(s, source, rightward):
-        send(
-            tok.at[s, source],
-            tok.at[s, source],
-            tok_sent.at[0 if rightward else 1, source],
-            tok_got.at[s, source],
-            {"row": jnp.minimum(me + 1, n_row - 1) if rightward else jnp.maximum(me - 1, 0)},
-        )
+    low = 2 * me < n_row
+    outward = jnp.where(low, -1, 1)
+    near = jnp.minimum(me, n_row - 1 - me)
+
+    def nearest(j):
+        step = (j + 1) // 2
+        both = jnp.where(low == (j % 2 == 1), -step, step)
+        one = jnp.where(low, j - near, near - j)
+        return me + jnp.where(j <= 2 * near, both, one)
+
+    def push_tokens(s, source, way):
+        target = me + way
+
+        @pl.when(jnp.logical_and(target >= 0, target < n_row))
+        def _():
+            send(
+                tok.at[s, source],
+                tok.at[s, source],
+                tok_sent.at[(way + 1) // 2, source],
+                tok_got.at[s, source],
+                {"row": jnp.clip(target, 0, n_row - 1)},
+            )
 
     def send_tokens(s):
-        @pl.when(has_right)
-        def _():
-            push_tokens(s, me, True)
-
-        @pl.when(has_left)
-        def _():
-            push_tokens(s, me, False)
+        push_tokens(s, me, -outward)
+        push_tokens(s, me, outward)
 
     def take_tokens(s, distance):
-        @pl.when(me >= distance)
-        def _():
-            source = jnp.maximum(me - distance, 0)
-            arrive(tok.at[s, source], tok_got.at[s, source])
-
-            @pl.when(has_right)
+        for way in (outward, -outward):
+            source = me + way * distance
+
+            @pl.when(jnp.logical_and(source >= 0, source < n_row))
             def _():
-                push_tokens(s, source, True)
-
-        @pl.when(me + distance < n_row)
-        def _():
-            source = jnp.minimum(me + distance, n_row - 1)
-            arrive(tok.at[s, source], tok_got.at[s, source])
-
-            @pl.when(has_left)
-            def _():
-                push_tokens(s, source, False)
+                place = jnp.clip(source, 0, n_row - 1)
+                arrive(tok.at[s, place], tok_got.at[s, place])
+                push_tokens(s, place, -way)
 
     def bias_part(target):
         return bias_send.at[
@@ -294,8 +296,7 @@
     scale = 1.0 / math.sqrt(HEAD_DIM)
 
     def project(sources, chosen=slice(None)):
-        rows = tok[chosen, sources].reshape(-1, width).astype(jnp.float32)
-        normed = normalize(rows, token_gain[...]).astype(jnp.bfloat16)
+        normed = tok[chosen, sources].reshape(-1, width)
         for index, target in enumerate((query, key, value)):
             done = lax.dot_general(
                 normed, qkv[index], (((1,), (1,)), ((), ())), preferred_element_type=jnp.float32
@@ -327,14 +328,22 @@
         ).astype(jnp.bfloat16)
         attended[s] = mixed.reshape(n_row, token_rows, local_width)
 
-    def give(s):
-        for d in range(1, n_row):
-            target = row_peer(d)
-            send(attended.at[s, target], heads_in.at[me * samples + s], sent.at[0], att_got.at[0], {"row": target})
-        heads_in[me * samples + s] = attended[s, me]
-
-    def take_attended():
-        arrive(heads_in.at[pl.ds(0, (n_row - 1) * samples)], att_got.at[0])
+    def give(first, last):
+        for j in range(n_row - 1, 0, -1):
+            target = nearest(j)
+            for s in range(first, last):
+                send(
+                    attended.at[s, target],
+                    heads_in.at[me * samples + s],
+                    sent.at[0],
+                    att_got.at[me],
+                    {"row": target},
+                )
+        for s in range(first, last):
+            heads_in[me * samples + s] = attended[s, me]
+
+    def take_attended(source):
+        arrive(heads_in.at[pl.ds(source * samples, samples)], att_got.at[source])
 
     def build_bias():
         lanes_at = lax.broadcasted_iota(jnp.int32, (part_rows, LANES), 1)
@@ -362,10 +371,15 @@
     everything = slice(None)
     with mark("tokload"):
         loads["tok"].wait()
+        loads["token_gain"].wait()
+    with mark("norm"):
+        rows = own[...].reshape(samples * token_rows, width).astype(jnp.float32)
+        normed = normalize(rows, token_gain[...]).astype(jnp.bfloat16)
+        tok[:, me] = normed.reshape(samples, token_rows, width)
     with mark("barrier"):
         await_greetings(barrier)
 
-    early = 2
+    early = min(2, samples)
     for s in range(early):
         send_tokens(s)
 
@@ -412,7 +426,7 @@
             await_greetings(greeting.at[r])
 
     with mark("loads"):
-        for name in ("ow", "qkv", "token_gain", "valid"):
+        for name in ("ow", "qkv", "valid"):
             loads[name].wait()
     send_bias()
     own_bias.start()
@@ -429,10 +443,10 @@
             project(me)
 
     def step(distance):
-        for s in range(samples):
+        for s in range(early if distance == 1 else 0, samples):
             with mark("tokens"):
                 take_tokens(s, distance)
-            if distance == 1 and s == 1:
+            if distance == 1 and s == min(3, samples - 1):
 
                 @pl.when(relay)
                 def _():
@@ -449,6 +463,11 @@
         with mark("bias0"):
             for k in range(1, n_row):
                 pass_bias(k)
+
+    if n_row > 2:
+        with mark("tokens0"):
+            for s in range(early):
+                take_tokens(s, 1)
 
     @pl.when(relay)
     def _():
@@ -483,8 +502,7 @@
             for s in range(first, last):
                 attend(s)
         with mark("give"):
-            for s in range(first, last):
-                give(s)
+            give(first, last)
 
     batch = max(samples // 2, 1)
     batches = [(first, min(first + batch, samples)) for first in range(0, samples, batch)]
@@ -520,17 +538,23 @@
             for k in range(1, n_row):
                 take_ow(k)
 
-    with mark("attwait"):
-        take_attended()
-
-    with mark("product"):
-        result = tok[:, me].reshape(samples * token_rows, width).astype(jnp.float32)
-        product = None
-        for r in range(n_row):
-            flat = heads_in[r * samples : (r + 1) * samples].reshape(samples * token_rows, local_width)
-            term = jnp.dot(flat, ow[r], preferred_element_type=jnp.float32)
-            product = term if product is None else product + term
-        out[...] = (result + product).astype(out.dtype).reshape(samples, token_rows, width)
+    def term(source):
+        flat = heads_in[pl.ds(source * samples, samples)].reshape(samples * token_rows, local_width)
+        return jnp.dot(flat, ow[source], preferred_element_type=jnp.float32)
+
+    with mark("product0"):
+        flat_shape = (samples * token_rows, width)
+        total_sum[...] = own[...].reshape(flat_shape).astype(jnp.float32) + term(me)
+    for j in range(1, n_row):
+        source = nearest(j)
+        with mark("attwait"):
+            take_attended(source)
+        with mark("product"):
+            if j < n_row - 1:
+                total_sum[...] += term(source)
+            else:
+                result = total_sum[...] + term(source)
+                out[...] = result.astype(out.dtype).reshape(samples, token_rows, width)
 
     with mark("fin"):
         for source in range(n_row):
@@ -538,7 +562,7 @@
 
                 @pl.when(jnp.logical_and(source <= me, has_right) if rightward else jnp.logical_and(source >= me, has_left))
                 def _():
-                    awaiting(tok.at[:, source], tok_sent.at[0 if rightward else 1, source]).wait_send()
+                    awaiting(tok.at[:, source], tok_sent.at[1 if rightward else 0, source]).wait_send()
 
         awaiting(bias_recv.at[pl.ds(0, n_row * n_plane - 1)], sent.at[1]).wait_send()
         awaiting(attended.at[:, pl.ds(0, n_row - 1)], sent.at[0]).wait_send()
@@ -592,6 +616,7 @@
             pltpu.VMEM(bias_weight.shape[::-1], bf16),
             pltpu.VMEM(token_gain.shape, f32),
             pltpu.VMEM((3, local_width, width), bf16),
+            pltpu.VMEM(tokens.shape, bf16),
             pltpu.VMEM((samples, n_row, token_rows, width), bf16),
             pltpu.VMEM((n_row, out_rows, width), bf16),
             pltpu.VMEM((heads * stripes, LANES), f32),
@@ -602,13 +627,14 @@
             pltpu.VMEM((samples, n_row, token_rows, local_width), bf16),
             pltpu.VMEM((samples, n_row, token_rows, local_width), bf16),
             pltpu.VMEM((n_row * samples, token_rows, local_width), bf16),
+            pltpu.VMEM((samples * token_rows, width), f32),
             dma((12,)),
             dma((samples, n_row)),
             dma((2, n_row)),
             dma((n_row,)),
             dma((3, n_row - 1)),
             dma((max(n_samp - 1, 1),)),
-            dma((1,)),
+            dma((n_row,)),
             dma((3,)),
             pltpu.SemaphoreType.REGULAR((max(n_row - 2, 2),)),
         ],

time: 29.3 us -> 28.8 us (0.983)
  Pallas kernels: 27.8 us -> 27.3 us
    pallas_call x1, Pallas kernels: 27.8 us -> 27.3 us  [per_device(): pl.pallas_call(functools.partial(kernel, axes, cuts), out_shape=jax.Shape...]
where the time goes in v3:
time: 28.8 us; the launch traced here: 28.7 us
  Pallas kernels  27.3 us (95%)
  local copies, waits for them, and re-layouts  0.68 us (2%)
  between operations  0.66 us (2%)
    pallas_call x1, Pallas kernels, per_device(): pl.pallas_call(functools.partial(kernel, axes, cuts), out_shape=jax.Shape...  27.3 us
    unnamed x1, local copies, waits for them, and re-layouts  0.68 us

profile of v3, /device:TPU:1, one launch (start us, length us, event | category | flops | bytes accessed | tf_op | source)
XLA Modules:
  0.0 28.7 jit_solution(2801703014702016868)
XLA Ops:
  0.7 27.3 %shard_map.100 = bf16[4,32,768]{2,1,0:T(8,128)(2,1)S(1)} custom-call(s32[128]{0:T(128)} %asym_hbm.1, s32[1]{0:T(128)S(6)} %copy.12.valid_hbm, bf16[32,32,128]{2,1,0:T(8,128)(2,1)} %pair_hbm.1, bf16[128,128]{1,0:T(8,128)(2,1)} %rel_hbm.1, f32[1,128]{1,0:T(1,128)} %bitcast.5, bf16[16,128]{1,0:T(8,128)(2,1)} %bitcast.4, bf16[4,32,768]{2,1,0:T(8,128)(2,1)} %tokens_hbm.1, ...), custom_call_target="tpu_custom_call" | custom-call | tf_op jit(solution)/shard_map/pallas_call | solution.py:605
  28.0 0.7 %copy.13 = bf16[4,32,768]{2,1,0:T(8,128)(2,1)} copy(bf16[4,32,768]{2,1,0:T(8,128)(2,1)S(1)} %shard_map.100) | data formatting | bytes 393216

commit v4 on v3

--- a/solution.py
+++ b/solution.py
@@ -180,34 +180,36 @@
 
     def send_ow():
         for k in range(1, n_row):
-            send(ow_piece(me, 0, 0), ow_piece(me, 0, 0), sent.at[2], ow_got.at[0, k - 1], {"row": row_peer(k)})
+            send(ow_piece(me, 0, 0), ow_piece(me, 0, 0), sent.at[2], ow_got.at[k - 1], {"row": row_peer(k)})
 
     def pair_ow(k, a, b):
         piece = ow_piece(row_source(k), a, b)
         for e in range(1, n_samp):
             device = {"samp": lax.rem(samp + e, n_samp)}
-            send(piece, piece, ow_sent.at[e - 1], ow_got.at[2, k - 1], device)
+            send(piece, piece, ow_sent.at[e - 1], ow_got.at[n_row], device)
 
     def spread_ow(k):
         piece = ow_piece(row_source(k), 0, 0)
-        arrive(piece, ow_got.at[0, k - 1])
+        arrive(piece, ow_got.at[k - 1])
         for a, b in chips[1:]:
             device = {
                 name: lax.rem(spot + step, size)
                 for name, spot, step, size in (("job", job, a, n_job), ("col", col, b, n_col))
                 if step
             }
-            send(piece, piece, sent.at[2], ow_got.at[1, k - 1], device)
+            send(piece, piece, sent.at[2], ow_got.at[n_row - 1], device)
         pair_ow(k, 0, 0)
 
-    def collect_ow(k):
+    def collect_ow():
         if pieces > 1:
-            arrive(ow.at[row_source(k), pl.ds(0, out_rows - out_rows // pieces)], ow_got.at[1, k - 1])
-            for a, b in chips[1:]:
-                pair_ow(k, a, b)
-
-    def take_ow(k):
-        arrive(ow.at[row_source(k)], ow_got.at[2, k - 1])
+            others = ow.at[pl.ds(0, n_row - 1), pl.ds(0, out_rows - out_rows // pieces)]
+            arrive(others, ow_got.at[n_row - 1])
+            for k in range(1, n_row):
+                for a, b in chips[1:]:
+                    pair_ow(k, a, b)
+
+    def take_ow():
+        arrive(ow.at[pl.ds(0, n_row - 1)], ow_got.at[n_row])
 
     low = 2 * me < n_row
     outward = jnp.where(low, -1, 1)
@@ -227,7 +229,7 @@
             send(
                 tok.at[s, source],
                 tok.at[s, source],
-                tok_sent.at[(way + 1) // 2, source],
+                tok_sent.at[(way + 1) // 2],
                 tok_got.at[s, source],
                 {"row": jnp.clip(target, 0, n_row - 1)},
             )
@@ -285,7 +287,7 @@
             arrive(bias_recv.at[pl.ds(0, n_row * (n_plane - 1))], bias_got.at[n_row - 1])
 
     own_bias = pltpu.make_async_copy(
-        bias_part(me), bias_recv.at[me * n_plane + plane], local_sem.at[11]
+        bias_part(me), bias_recv.at[me * n_plane + plane], local_sem.at[10]
     )
 
     head_of_lane = lax.broadcasted_iota(jnp.int32, (total, local_width), 1)
@@ -487,8 +489,7 @@
         @pl.when(relay)
         def _():
             with mark("ow1"):
-                for k in range(1, n_row):
-                    collect_ow(k)
+                collect_ow()
 
     def prepare_bias():
         with mark("bias2"):
@@ -517,8 +518,7 @@
             with mark("project"):
                 project(n_row - 1 - me, slice(first, last))
             finish_samples(first, last)
-            if first == 0:
-                relay_ow()
+        relay_ow()
 
     @pl.when(jnp.logical_not(edge))
     def _():
@@ -535,8 +535,7 @@
     @pl.when(jnp.logical_not(relay))
     def _():
         with mark("ow3"):
-            for k in range(1, n_row):
-                take_ow(k)
+            take_ow()
 
     def term(source):
         flat = heads_in[pl.ds(source * samples, samples)].reshape(samples * token_rows, local_width)
@@ -557,12 +556,14 @@
                 out[...] = result.astype(out.dtype).reshape(samples, token_rows, width)
 
     with mark("fin"):
-        for source in range(n_row):
-            for rightward in (True, False):
-
-                @pl.when(jnp.logical_and(source <= me, has_right) if rightward else jnp.logical_and(source >= me, has_left))
-                def _():
-                    awaiting(tok.at[:, source], tok_sent.at[1 if rightward else 0, source]).wait_send()
+        for row in range(n_row):
+
+            @pl.when(me == row)
+            def _():
+                if row < n_row - 1:
+                    awaiting(tok.at[:, pl.ds(0, row + 1)], tok_sent.at[1]).wait_send()
+                if row > 0:
+                    awaiting(tok.at[:, pl.ds(0, n_row - row)], tok_sent.at[0]).wait_send()
 
         awaiting(bias_recv.at[pl.ds(0, n_row * n_plane - 1)], sent.at[1]).wait_send()
         awaiting(attended.at[:, pl.ds(0, n_row - 1)], sent.at[0]).wait_send()
@@ -628,11 +629,11 @@
             pltpu.VMEM((samples, n_row, token_rows, local_width), bf16),
             pltpu.VMEM((n_row * samples, token_rows, local_width), bf16),
             pltpu.VMEM((samples * token_rows, width), f32),
-            dma((12,)),
+            dma((11,)),
             dma((samples, n_row)),
-            dma((2, n_row)),
+            dma((2,)),
             dma((n_row,)),
-            dma((3, n_row - 1)),
+            dma((n_row + 1,)),
             dma((max(n_samp - 1, 1),)),
             dma((n_row,)),
             dma((3,)),

time: 28.8 us -> 29.5 us (1.024)
  the two profiles are of different devices: /device:TPU:1 before, /device:TPU:0 now
where the time goes in v4:
time: 29.5 us; the launch traced here: 29.3 us
  Pallas kernels  28 us (95%)
  local copies, waits for them, and re-layouts  0.68 us (2%)
  between operations  0.66 us (2%)
    pallas_call x1, Pallas kernels, per_device(): pl.pallas_call(functools.partial(kernel, axes, cuts), out_shape=jax.Shape...  28 us
    unnamed x1, local copies, waits for them, and re-layouts  0.68 us

profile of v4, /device:TPU:0, one launch (start us, length us, event | category | flops | bytes accessed | tf_op | source)
XLA Modules:
  0.0 29.3 jit_solution(3945052194899072962)
XLA Ops:
  0.7 28.0 %shard_map.100 = bf16[4,32,768]{2,1,0:T(8,128)(2,1)S(1)} custom-call(s32[128]{0:T(128)} %asym_hbm.1, s32[1]{0:T(128)S(6)} %copy.12.valid_hbm, bf16[32,32,128]{2,1,0:T(8,128)(2,1)} %pair_hbm.1, bf16[128,128]{1,0:T(8,128)(2,1)} %rel_hbm.1, f32[1,128]{1,0:T(1,128)} %bitcast.5, bf16[16,128]{1,0:T(8,128)(2,1)} %bitcast.4, bf16[4,32,768]{2,1,0:T(8,128)(2,1)} %tokens_hbm.1, ...), custom_call_target="tpu_custom_call" | custom-call | tf_op jit(solution)/shard_map/pallas_call | solution.py:606
  28.6 0.7 %copy.13 = bf16[4,32,768]{2,1,0:T(8,128)(2,1)} copy(bf16[4,32,768]{2,1,0:T(8,128)(2,1)S(1)} %shard_map.100) | data formatting | bytes 393216

commit v5 on v4

--- a/solution.py
+++ b/solution.py
@@ -518,7 +518,8 @@
             with mark("project"):
                 project(n_row - 1 - me, slice(first, last))
             finish_samples(first, last)
-        relay_ow()
+            if first == 0:
+                relay_ow()
 
     @pl.when(jnp.logical_not(edge))
     def _():

time: 29.5 us -> 28.7 us (0.973)
  the two profiles are of different devices: /device:TPU:0 before, /device:TPU:1 now
where the time goes in v5:
time: 28.7 us; the launch traced here: 28.6 us
  Pallas kernels  27.2 us (95%)
  local copies, waits for them, and re-layouts  0.68 us (2%)
  between operations  0.66 us (2%)
    pallas_call x1, Pallas kernels, per_device(): pl.pallas_call(functools.partial(kernel, axes, cuts), out_shape=jax.Shape...  27.2 us
    unnamed x1, local copies, waits for them, and re-layouts  0.68 us

profile of v5, /device:TPU:1, one launch (start us, length us, event | category | flops | bytes accessed | tf_op | source)
XLA Modules:
  0.0 28.6 jit_solution(446744096561308495)
XLA Ops:
  0.7 27.2 %shard_map.100 = bf16[4,32,768]{2,1,0:T(8,128)(2,1)S(1)} custom-call(s32[128]{0:T(128)} %asym_hbm.1, s32[1]{0:T(128)S(6)} %copy.12.valid_hbm, bf16[32,32,128]{2,1,0:T(8,128)(2,1)} %pair_hbm.1, bf16[128,128]{1,0:T(8,128)(2,1)} %rel_hbm.1, f32[1,128]{1,0:T(1,128)} %bitcast.5, bf16[16,128]{1,0:T(8,128)(2,1)} %bitcast.4, bf16[4,32,768]{2,1,0:T(8,128)(2,1)} %tokens_hbm.1, ...), custom_call_target="tpu_custom_call" | custom-call | tf_op jit(solution)/shard_map/pallas_call | solution.py:607
  27.9 0.7 %copy.13 = bf16[4,32,768]{2,1,0:T(8,128)(2,1)} copy(bf16[4,32,768]{2,1,0:T(8,128)(2,1)S(1)} %shard_map.100) | data formatting | bytes 393216

commit v6 on v5

--- a/solution.py
+++ b/solution.py
@@ -179,7 +179,7 @@
     chips = [(a, b) for a in range(p_job) for b in range(p_col)]
 
     def send_ow():
-        for k in range(1, n_row):
+        for k in range(n_row - 1, 0, -1):
             send(ow_piece(me, 0, 0), ow_piece(me, 0, 0), sent.at[2], ow_got.at[k - 1], {"row": row_peer(k)})
 
     def pair_ow(k, a, b):
@@ -267,7 +267,7 @@
             )
 
     def send_bias():
-        for k in range(1, n_row):
+        for k in range(n_row - 1, 0, -1):
             target = row_peer(k)
             send(
                 bias_part(target),

time: 28.7 us -> 28.8 us (level)
  no operation moved by 1% of the time
where the time goes in v6:
time: 28.8 us; the launch traced here: 28.7 us
  Pallas kernels  27.3 us (95%)
  local copies, waits for them, and re-layouts  0.68 us (2%)
  between operations  0.66 us (2%)
    pallas_call x1, Pallas kernels, per_device(): pl.pallas_call(functools.partial(kernel, axes, cuts), out_shape=jax.Shape...  27.3 us
    unnamed x1, local copies, waits for them, and re-layouts  0.68 us

profile of v6, /device:TPU:1, one launch (start us, length us, event | category | flops | bytes accessed | tf_op | source)
XLA Modules:
  0.0 28.7 jit_solution(9460962774247557936)
XLA Ops:
  0.7 27.3 %shard_map.100 = bf16[4,32,768]{2,1,0:T(8,128)(2,1)S(1)} custom-call(s32[128]{0:T(128)} %asym_hbm.1, s32[1]{0:T(128)S(6)} %copy.12.valid_hbm, bf16[32,32,128]{2,1,0:T(8,128)(2,1)} %pair_hbm.1, bf16[128,128]{1,0:T(8,128)(2,1)} %rel_hbm.1, f32[1,128]{1,0:T(1,128)} %bitcast.5, bf16[16,128]{1,0:T(8,128)(2,1)} %bitcast.4, bf16[4,32,768]{2,1,0:T(8,128)(2,1)} %tokens_hbm.1, ...), custom_call_target="tpu_custom_call" | custom-call | tf_op jit(solution)/shard_map/pallas_call | solution.py:607
  28.0 0.7 %copy.13 = bf16[4,32,768]{2,1,0:T(8,128)(2,1)} copy(bf16[4,32,768]{2,1,0:T(8,128)(2,1)S(1)} %shard_map.100) | data formatting | bytes 393216
